TPU v7x, 32 devices: a whole 2x2x4 slice. The times are simulated.
32 devices in a mesh: dp: 4 (over y, x), eng: 2 (over core), tp: 4 (over z).
Axes of the slice: x: 2, y: 2, z: 4, core: 2. Of those that a mesh axis runs over, the one named last changes fastest.
Arguments:
- grad_parts: bfloat16 [4, 4, 1024, 14336], P('dp', 'tp', None, 'eng'), may hold values from -24 to 24
- master: float32 [4, 1024, 14336], P('tp', 'dp', 'eng'), may hold values from -0.09375 to 0.09375
- first_moment: float32 [4, 1024, 14336], P('tp', 'dp', 'eng'), may hold values from -12 to 12
- second_moment: float32 [4, 1024, 14336], P('tp', 'dp', 'eng'), may hold values from 4 to 256
- adam_step: int32 [1], replicated, may hold values from 1 to 999
- rank_map: int32 [4], replicated, may hold values from 0 to 3, each once
Outputs:
- new_master: float32 [4, 1024, 14336], P('tp', 'dp', 'eng')
- new_first: float32 [4, 1024, 14336], P('tp', 'dp', 'eng')
- new_second: float32 [4, 1024, 14336], P('tp', 'dp', 'eng')
- rollout: bfloat16 [4, 1024, 2, 4, 1792], P(None, 'dp', None, 'tp')
Inputs may be any that keep to these rules, and one draw needn't show every extreme that they name: `rank_map`: each of 0 to 3 appears once.
All inputs are finite; a program needn't handle non-finite values.
Results may differ from a plain program's by a relative error of at most 0.001.
Values may be sent and summed in bfloat16 or wider, within the bound.
A program may use at most 192 MiB of HBM per device.

v0:
```python
import functools
import jax
import jax.numpy as jnp
from jax import lax
from jax.experimental import pallas as pl
from jax.experimental.pallas import tpu as pltpu
from jax.sharding import PartitionSpec as P

beta_one = 0.9
beta_two = 0.95
rate_value = 0.001
decay_value = 0.01
eps_value = 1e-08

ROWS = 16
AHEAD = 3
STRIP = 256
TOP = 32767.0
TINY = 1e-30
MESH = pl.DeviceIdType.MESH


def corrections(adam_step):
    count = adam_step[0].astype(jnp.float32)
    return 1.0 - jnp.power(beta_one, count), 1.0 - jnp.power(beta_two, count)


def plain_shards(grad_parts, master, first_moment, second_moment, adam_step, rank_map):
    summed = lax.psum_scatter(grad_parts.astype(jnp.float32), "dp", scatter_dimension=2, tiled=True)
    summed = summed.reshape(master.shape)
    fix_one, fix_two = corrections(adam_step)
    new_first = beta_one * first_moment + (1.0 - beta_one) * summed
    new_second = beta_two * second_moment + (1.0 - beta_two) * summed * summed
    first_hat = new_first / fix_one
    second_hat = new_second / fix_two
    new_master = master - rate_value * (
        first_hat / (jnp.sqrt(second_hat) + eps_value) + decay_value * master
    )
    row_count = master.shape[1]
    ranks = lax.axis_size("tp")
    block_width = master.shape[2] // ranks
    piece = new_master.astype(jnp.bfloat16).reshape(1, row_count, 1, ranks, block_width)
    ordered = jnp.take(piece, rank_map, axis=3)
    placed = lax.all_to_all(ordered, "tp", split_axis=3, concat_axis=0, tiled=True)
    rollout = lax.all_gather(placed, "eng", axis=2, tiled=True)
    return (new_master, new_first, new_second, rollout)


def pack_sum(near, far, packed, scale):
    tiles = packed.shape[1] // 128
    tops = [jnp.zeros((8, 128), jnp.float32) for _ in range(4)]
    for tile in range(tiles):
        columns = pl.ds(tile * 128, 128)
        size = jnp.abs(near[:, columns].astype(jnp.float32) + far[:, columns].astype(jnp.float32))
        for part in range(ROWS // 8):
            slot = (2 * tile + part) % 4
            tops[slot] = jnp.maximum(tops[slot], size[8 * part : 8 * part + 8])
    top = jnp.maximum(jnp.maximum(tops[0], tops[1]), jnp.maximum(tops[2], tops[3]))
    top = jnp.maximum(top, TINY)
    scale[...] = top * (1.0 / TOP)
    factor = jnp.concatenate([TOP / top] * (ROWS // 8), axis=0)
    for tile in range(tiles):
        columns = pl.ds(tile * 128, 128)
        value = near[:, columns].astype(jnp.float32) + far[:, columns].astype(jnp.float32)
        packed[:, columns] = jnp.round(value * factor).astype(jnp.int32).astype(jnp.int16)


def kernel(
    ranks, order, scales, grad, master, first, second,
    new_master, new_first, new_second, both,
    rxa, rxb, txa, txb, tsa, tsb, r2a, r2b, rsa, rsb, zs, zr,
    own, side_a, side_b, old, new, held,
    p1_send, p1_recv, p2_send, p2_recv, z_send, z_recv, f_send, f_recv,
    own_sem, side_sem, old_sem, new_sem, keep_sem,
):
    columns = grad.shape[2]
    half = columns // 2
    width = columns // ranks
    chunks = rxa.shape[0]
    me, tp, eng = (lax.axis_index(a) for a in ("dp", "tp", "eng"))
    at_x = me + 1 - 2 * (me % 2)
    at_y = (me + 2) % 4
    at_d = 3 - me
    left, right = pl.ds(0, half), pl.ds(half, half)
    states, outs = (master, first, second), (new_master, new_first, new_second)

    def rows_of(chunk):
        return pl.ds(pl.multiple_of(chunk * ROWS, ROWS), ROWS)

    def remote(src, dst, send, recv, **where):
        return pltpu.make_async_remote_copy(
            src_ref=src, dst_ref=dst, send_sem=send, recv_sem=recv, device_id=where, device_id_type=MESH
        )

    def first_stage(c):
        rows = rows_of(c)
        return [
            remote(grad.at[at_d, rows, left], rxa.at[c, 1], p1_send.at[c, 0], p1_recv.at[c, 0], dp=at_x),
            remote(grad.at[at_d, rows, right], rxb.at[c, 1], p1_send.at[c, 1], p1_recv.at[c, 1], dp=at_y),
            remote(grad.at[at_x, rows, left], rxa.at[c, 0], p1_send.at[c, 2], p1_recv.at[c, 2], dp=at_x),
            remote(grad.at[at_y, rows, right], rxb.at[c, 0], p1_send.at[c, 3], p1_recv.at[c, 3], dp=at_y),
        ]

    def second_stage(c):
        return [
            remote(txa.at[c], r2a.at[c], p2_send.at[c, 0], p2_recv.at[c, 0], dp=at_y),
            remote(tsa.at[c], rsa.at[c], p2_send.at[c, 1], p2_recv.at[c, 1], dp=at_y),
            remote(txb.at[c], r2b.at[c], p2_send.at[c, 2], p2_recv.at[c, 2], dp=at_x),
            remote(tsb.at[c], rsb.at[c], p2_send.at[c, 3], p2_recv.at[c, 3], dp=at_x),
        ]

    def publish(c):
        return [
            remote(zs.at[c, hop], zr.at[hop, c], z_send.at[c, hop], z_recv.at[c, hop], tp=(tp + hop) % ranks)
            for hop in range(1, ranks)
        ]

    def forward(c, hop):
        src = zs.at[c, 0] if hop == 0 else zr.at[hop, c]
        place = both.at[eng, (tp + ranks - hop) % ranks, rows_of(c)]
        return (
            remote(src, place, f_send.at[c, hop], f_recv.at[c, hop], eng=1 - eng),
            pltpu.make_async_copy(src, place, keep_sem.at[c, hop]),
        )

    def arrived(c, hop):
        place = both.at[1 - eng, (tp + ranks - hop) % ranks, rows_of(c)]
        return remote(place, place, f_send.at[c, hop], f_recv.at[c, hop], eng=1 - eng)

    def load_own(c):
        return [pltpu.make_async_copy(grad.at[me, rows_of(c)], own.at[c % 2], own_sem.at[c % 2])]

    def load_side(c):
        return [
            pltpu.make_async_copy(grad.at[at_y, rows_of(c), left], side_a.at[c % 2], side_sem.at[c % 2, 0]),
            pltpu.make_async_copy(grad.at[at_x, rows_of(c), right], side_b.at[c % 2], side_sem.at[c % 2, 1]),
        ]

    def load_old(c):
        return [
            pltpu.make_async_copy(states[i].at[rows_of(c)], old.at[c % 2, i], old_sem.at[c % 2, i]) for i in range(3)
        ]

    def store_new(c):
        return [
            pltpu.make_async_copy(new.at[c % 2, i], outs[i].at[rows_of(c)], new_sem.at[c % 2, i]) for i in range(3)
        ]

    def start(copies):
        for copy in copies:
            copy.start()

    def wait(copies):
        for copy in copies:
            copy.wait()

    def wait_recv(copies):
        for copy in copies:
            copy.wait_recv()

    for c in range(2):
        start(load_side(c) + load_own(c) + load_old(c))
    barrier = pltpu.get_barrier_semaphore()
    for where in (
        [{"dp": at_x}, {"dp": at_y}, {"eng": 1 - eng}] + [{"tp": (tp + hop) % ranks} for hop in range(1, ranks)]
    ):
        pl.semaphore_signal(barrier, inc=1, device_id=where, device_id_type=MESH)
    pl.semaphore_wait(barrier, 2 + ranks)
    for c in range(AHEAD):
        start(first_stage(c))

    def reduce_side(c):
        slot = c % 2
        wait(load_side(c))
        copies = first_stage(c)
        copies[0].wait_recv()
        pack_sum(side_a.at[slot], rxa.at[c, 1], txa.at[c], tsa.at[c])
        start(second_stage(c)[:2])
        copies[1].wait_recv()
        pack_sum(side_b.at[slot], rxb.at[c, 1], txb.at[c], tsb.at[c])
        start(second_stage(c)[2:])

        @pl.when(c + 2 < chunks)
        def _():
            start(load_side(c + 2))

    def update(c):
        slot = c % 2
        wait(load_own(c) + load_old(c))
        wait_recv(first_stage(c)[2:])
        wait_recv(second_stage(c))

        @pl.when(c >= 2)
        def _():
            wait(store_new(c - 2))

        scale_one, scale_two = scales[0], scales[1]
        for strip in range(columns // STRIP):
            at = pl.ds(strip * STRIP, STRIP)
            side = strip * STRIP // half
            inner = pl.ds(strip * STRIP - side * half, STRIP)
            got, sums, units = ((rxa, r2a, rsa), (rxb, r2b, rsb))[side]
            unit = units[c]
            unit = jnp.concatenate([jnp.concatenate([unit] * (ROWS // 8), axis=0)] * (STRIP // 128), axis=1)
            summed = own[slot, :, at].astype(jnp.float32) + got[c, 0, :, inner].astype(jnp.float32)
            summed += sums[c, :, inner].astype(jnp.int32).astype(jnp.float32) * unit
            first_now = beta_one * old[slot, 1, :, at] + (1.0 - beta_one) * summed
            second_now = beta_two * old[slot, 2, :, at] + (1.0 - beta_two) * summed * summed
            was = old[slot, 0, :, at]
            step = (first_now * scale_one) / (jnp.sqrt(second_now * scale_two) + eps_value)
            now = was - rate_value * (step + decay_value * was)
            new[slot, 0, :, at] = now
            new[slot, 1, :, at] = first_now
            new[slot, 2, :, at] = second_now
            block = strip * STRIP // width
            held[block, :, pl.ds(strip * STRIP - block * width, STRIP)] = now.astype(jnp.bfloat16)
        start(store_new(c))
        for hop in range(ranks):
            zs[c, hop] = held[order[hop]]
        start(publish(c))
        start(forward(c, 0))

        @pl.when(c + 2 < chunks)
        def _():
            start(load_own(c + 2) + load_old(c + 2))

    def spread(c):
        copies = publish(c)
        for hop in range(1, ranks):
            copies[hop - 1].wait_recv()
            start(forward(c, hop))

    def body(s, carry):
        @pl.when(s + AHEAD < chunks)
        def _():
            start(first_stage(s + AHEAD))

        @pl.when(s < chunks)
        def _():
            reduce_side(s)

        @pl.when((s >= 1) & (s <= chunks))
        def _():
            update(s - 1)

        @pl.when(s >= 2)
        def _():
            spread(s - 2)

        return carry

    lax.fori_loop(0, chunks + 2, body, 0)

    def drain(c, carry):
        for copy in first_stage(c) + second_stage(c) + publish(c):
            copy.wait_send()
        for hop in range(ranks):
            away, keep = forward(c, hop)
            away.wait_send()
            keep.wait()
            arrived(c, hop).wait_recv()
        return carry

    lax.fori_loop(0, chunks, drain, 0)
    wait(store_new(chunks - 2) + store_new(chunks - 1))


def shards(grad_parts, master, first_moment, second_moment, adam_step, rank_map):
    replicas, ranks = lax.axis_size("dp"), lax.axis_size("tp")
    row_count, columns = master.shape[1], master.shape[2]
    half, width = columns // 2, columns // ranks
    chunks = row_count // ROWS
    me_tp = lax.axis_index("tp")
    grad = grad_parts.reshape(replicas, row_count, columns)
    states = [s.reshape(row_count, columns) for s in (master, first_moment, second_moment)]
    order = lax.dynamic_slice(jnp.concatenate([rank_map, rank_map]), (me_tp,), (ranks,))
    scales = jnp.stack([1.0 / value for value in corrections(adam_step)])
    smem, anywhere = pl.BlockSpec(memory_space=pltpu.SMEM), pl.BlockSpec(memory_space=pl.ANY)
    vmem, dma = pltpu.VMEM, pltpu.SemaphoreType.DMA
    short, brain, single = jnp.int16, jnp.bfloat16, jnp.float32
    *outs, both = pl.pallas_call(
        functools.partial(kernel, ranks),
        out_shape=[jax.ShapeDtypeStruct(s.shape, s.dtype) for s in states]
        + [jax.ShapeDtypeStruct((2, ranks, row_count, width), brain)],
        in_specs=[smem, smem] + [anywhere] * 4,
        out_specs=[anywhere] * 4,
        scratch_shapes=[
            vmem((chunks, 2, ROWS, half), brain),
            vmem((chunks, 2, ROWS, half), brain),
            vmem((chunks, ROWS, half), short),
            vmem((chunks, ROWS, half), short),
            vmem((chunks, 8, 128), single),
            vmem((chunks, 8, 128), single),
            vmem((chunks, ROWS, half), short),
            vmem((chunks, ROWS, half), short),
            vmem((chunks, 8, 128), single),
            vmem((chunks, 8, 128), single),
            vmem((chunks, ranks, ROWS, width), brain),
            vmem((ranks, chunks, ROWS, width), brain),
            vmem((2, ROWS, columns), brain),
            vmem((2, ROWS, half), brain),
            vmem((2, ROWS, half), brain),
            vmem((2, 3, ROWS, columns), single),
            vmem((2, 3, ROWS, columns), single),
            vmem((ranks, ROWS, width), brain),
            dma((chunks, 4)),
            dma((chunks, 4)),
            dma((chunks, 4)),
            dma((chunks, 4)),
            dma((chunks, ranks)),
            dma((chunks, ranks)),
            dma((chunks, ranks)),
            dma((chunks, ranks)),
            dma((2,)),
            dma((2, 2)),
            dma((2, 3)),
            dma((2, 3)),
            dma((chunks, ranks)),
        ],
        compiler_params=pltpu.CompilerParams(
            collective_id=0, has_side_effects=True, vmem_limit_bytes=48 * 1024 * 1024
        ),
        name="exchange",
    )(order, scales, grad, *states)
    rollout = jnp.transpose(both, (1, 2, 0, 3)).reshape(ranks, row_count, 2, 1, width)
    return (*(o.reshape(master.shape) for o in outs), rollout)


def solution(mesh):
    sizes = dict(mesh.shape)

    def step(grad_parts, master, *rest):
        columns = master.shape[2] // sizes["eng"]
        width = columns // sizes["tp"]
        rows = master.shape[1] // sizes["dp"]
        fits = sizes["dp"] == 4 and sizes["eng"] == 2 and width % STRIP == 0 and (columns // 2) % STRIP == 0
        fits = fits and rows % ROWS == 0 and rows // ROWS > AHEAD
        return jax.shard_map(
            shards if fits else plain_shards,
            mesh=mesh,
            in_specs=(
                P("dp", "tp", None, "eng"),
                P("tp", "dp", "eng"),
                P("tp", "dp", "eng"),
                P("tp", "dp", "eng"),
                P(),
                P(),
            ),
            out_specs=(
                P("tp", "dp", "eng"),
                P("tp", "dp", "eng"),
                P("tp", "dp", "eng"),
                P(None, "dp", None, "tp", None),
            ),
            check_vma=False,
        )(grad_parts, master, *rest)

    return step
```

profile of v0, /device:TPU:0, one launch (start us, length us, event | category | flops | bytes accessed | tf_op | source)
XLA Modules:
  0.0 178.1 jit_solution(12409245106594463553)
XLA Ops:
  1.4 0.1 pad_maximum_fusion.scales
  1.5 0.8 pad_add_fusion
  2.3 0.1 dynamic_slice.3.order
  2.4 147.1 %exchange.1 = (f32[256,7168]{1,0:T(8,128)}, f32[256,7168]{1,0:T(8,128)}, f32[256,7168]{1,0:T(8,128)}, bf16[2,4,256,1792]{3,2,1,0:T(8,128)(2,1)}) custom-call(s32[4]{0:T(128)S(1)} %dynamic_slice.3.order, f32[2]{0:T(128)S(1)} %pad_maximum_fusion.scales, bf16[4,256,7168]{2,1,0:T(8,128)(2,1)} %bitcast.10, f32[256,7168]{1,0:T(8,128)} %bitcast.17, ...), custom_call_target="tpu_custom_call" | custom-call | tf_op jit(solution)/shard_map/exchange/pallas_call | solution.py:281
  149.5 0.0 copy-start.1
  149.5 14.8 %copy.10 = bf16[4,256,2,1,1792]{4,2,3,1,0:T(2,128)(2,1)} copy(bf16[4,256,2,1,1792]{4,1,0,2,3:T(8,128)(2,1)} %bitcast.16) | data formatting | bytes 14680064
  164.3 0.0 copy-done.1
  164.3 0.0 copy-start
  164.3 0.0 slice-start
  164.3 3.7 %copy.15 = f32[1,256,7168]{2,1,0:T(8,128)} copy(f32[1,256,7168]{2,1,0:T(8,128)S(1)} %bitcast.15) | data formatting | bytes 14680064
  168.0 2.0 %copy-done = f32[256,7168]{1,0:T(8,128)S(1)} copy-done((f32[256,7168]{1,0:T(8,128)S(1)}, f32[256,7168]{1,0:T(8,128)}, u32[]{:S(2)}) %copy-start) | copy-done | bytes 7340056
  170.0 0.0 slice-start.1
  170.0 3.7 %copy.16 = f32[1,256,7168]{2,1,0:T(8,128)} copy(f32[1,256,7168]{2,1,0:T(8,128)S(1)} %bitcast.14) | data formatting | bytes 14680064
  173.8 0.0 slice-done
  173.8 1.3 slice-done.1
  175.0 3.0 %copy.17 = f32[1,256,7168]{2,1,0:T(8,128)} copy(f32[1,256,7168]{2,1,0:T(8,128)S(1)} %bitcast.13) | data formatting | bytes 14680064
  (1 shorter events, 0.0 us)
Async XLA Ops:
  149.5 14.8 %copy-start.1 = (f32[256,7168]{1,0:T(8,128)S(1)}, f32[256,7168]{1,0:T(8,128)}, u32[]{:S(2)}) copy-start(f32[256,7168]{1,0:T(8,128)} %get-tuple-element.8) | copy-start | bytes 22020100
  164.3 5.7 %copy-start = (f32[256,7168]{1,0:T(8,128)S(1)}, f32[256,7168]{1,0:T(8,128)}, u32[]{:S(2)}) copy-start(f32[256,7168]{1,0:T(8,128)} %get-tuple-element.9) | copy-start | bytes 22020100
  164.3 9.5 %slice-start = ((s8[7340032]{0:T(1024)(128)(4,1)}), s8[4194304]{0:T(1024)(128)(4,1)S(1)}, s32[]{:S(2)}) async-start(s8[7340032]{0:T(1024)(128)(4,1)} %bitcast.11), calls=%async_computation | async-start | bytes 8388608
  170.0 5.0 %slice-start.1 = ((s8[7340032]{0:T(1024)(128)(4,1)}), s8[3145728]{0:T(1024)(128)(4,1)S(1)}, s32[]{:S(2)}) async-start(s8[7340032]{0:T(1024)(128)(4,1)} %bitcast.11), calls=%async_computation.1 | async-start | bytes 6291456
where the time goes:
time: 178 us
  Pallas kernels  147 us (83%)
  local copies, waits for them, and re-layouts  28.6 us (16%)
    pallas_call x1, Pallas kernels, shards(): pl.pallas_call(functools.partial(kernel, ranks), out_shape=[jax.ShapeDtyp...  147 us
    unnamed x12, local copies, waits for them, and re-layouts  28.5 us

commit v1 on v0

--- a/solution.py
+++ b/solution.py
@@ -13,7 +13,7 @@
 eps_value = 1e-08
 
 ROWS = 16
-AHEAD = 3
+AHEAD = 2
 STRIP = 256
 TOP = 32767.0
 TINY = 1e-30
@@ -67,11 +67,11 @@
 
 def kernel(
     ranks, order, scales, grad, master, first, second,
-    new_master, new_first, new_second, both,
+    new_master, new_first, new_second, rollout,
     rxa, rxb, txa, txb, tsa, tsb, r2a, r2b, rsa, rsb, zs, zr,
-    own, side_a, side_b, old, new, held,
+    own, side_a, side_b, old, held,
     p1_send, p1_recv, p2_send, p2_recv, z_send, z_recv, f_send, f_recv,
-    own_sem, side_sem, old_sem, new_sem, keep_sem,
+    own_sem, side_sem, old_sem,
 ):
     columns = grad.shape[2]
     half = columns // 2
@@ -82,7 +82,7 @@
     at_y = (me + 2) % 4
     at_d = 3 - me
     left, right = pl.ds(0, half), pl.ds(half, half)
-    states, outs = (master, first, second), (new_master, new_first, new_second)
+    states = (master, first, second)
 
     def rows_of(chunk):
         return pl.ds(pl.multiple_of(chunk * ROWS, ROWS), ROWS)
@@ -109,23 +109,18 @@
             remote(tsb.at[c], rsb.at[c], p2_send.at[c, 3], p2_recv.at[c, 3], dp=at_x),
         ]
 
-    def publish(c):
-        return [
-            remote(zs.at[c, hop], zr.at[hop, c], z_send.at[c, hop], z_recv.at[c, hop], tp=(tp + hop) % ranks)
-            for hop in range(1, ranks)
-        ]
+    def publish(c, hop):
+        return remote(
+            zs.at[c, hop - 1], zr.at[eng, hop, c], z_send.at[c, hop], z_recv.at[c, hop], tp=(tp + hop) % ranks
+        )
 
     def forward(c, hop):
-        src = zs.at[c, 0] if hop == 0 else zr.at[hop, c]
-        place = both.at[eng, (tp + ranks - hop) % ranks, rows_of(c)]
-        return (
-            remote(src, place, f_send.at[c, hop], f_recv.at[c, hop], eng=1 - eng),
-            pltpu.make_async_copy(src, place, keep_sem.at[c, hop]),
-        )
-
-    def arrived(c, hop):
-        place = both.at[1 - eng, (tp + ranks - hop) % ranks, rows_of(c)]
-        return remote(place, place, f_send.at[c, hop], f_recv.at[c, hop], eng=1 - eng)
+        block = zr.at[eng, hop, c]
+        return remote(block, block, f_send.at[c, hop], f_recv.at[c, hop], eng=1 - eng)
+
+    def arrival(c, hop):
+        block = zr.at[1 - eng, hop, c]
+        return remote(block, block, f_send.at[c, hop], f_recv.at[c, hop], eng=1 - eng)
 
     def load_own(c):
         return [pltpu.make_async_copy(grad.at[me, rows_of(c)], own.at[c % 2], own_sem.at[c % 2])]
@@ -139,11 +134,6 @@
     def load_old(c):
         return [
             pltpu.make_async_copy(states[i].at[rows_of(c)], old.at[c % 2, i], old_sem.at[c % 2, i]) for i in range(3)
-        ]
-
-    def store_new(c):
-        return [
-            pltpu.make_async_copy(new.at[c % 2, i], outs[i].at[rows_of(c)], new_sem.at[c % 2, i]) for i in range(3)
         ]
 
     def start(copies):
@@ -185,14 +175,10 @@
             start(load_side(c + 2))
 
     def update(c):
-        slot = c % 2
+        slot, rows = c % 2, rows_of(c)
         wait(load_own(c) + load_old(c))
         wait_recv(first_stage(c)[2:])
         wait_recv(second_stage(c))
-
-        @pl.when(c >= 2)
-        def _():
-            wait(store_new(c - 2))
 
         scale_one, scale_two = scales[0], scales[1]
         for strip in range(columns // STRIP):
@@ -209,26 +195,31 @@
             was = old[slot, 0, :, at]
             step = (first_now * scale_one) / (jnp.sqrt(second_now * scale_two) + eps_value)
             now = was - rate_value * (step + decay_value * was)
-            new[slot, 0, :, at] = now
-            new[slot, 1, :, at] = first_now
-            new[slot, 2, :, at] = second_now
+            new_master[rows, at] = now
+            new_first[rows, at] = first_now
+            new_second[rows, at] = second_now
             block = strip * STRIP // width
             held[block, :, pl.ds(strip * STRIP - block * width, STRIP)] = now.astype(jnp.bfloat16)
-        start(store_new(c))
+        for hop in range(1, ranks):
+            zs[c, hop - 1] = held[order[hop]]
+            publish(c, hop).start()
+        zr[eng, 0, c] = held[order[0]]
+        forward(c, 0).start()
+
+        @pl.when(c + 2 < chunks)
+        def _():
+            start(load_own(c + 2) + load_old(c + 2))
+
+    def spread(c):
+        for hop in range(1, ranks):
+            publish(c, hop).wait_recv()
+            forward(c, hop).start()
+
+    def merge(c):
         for hop in range(ranks):
-            zs[c, hop] = held[order[hop]]
-        start(publish(c))
-        start(forward(c, 0))
-
-        @pl.when(c + 2 < chunks)
-        def _():
-            start(load_own(c + 2) + load_old(c + 2))
-
-    def spread(c):
-        copies = publish(c)
-        for hop in range(1, ranks):
-            copies[hop - 1].wait_recv()
-            start(forward(c, hop))
+            arrival(c, hop).wait_recv()
+            rollout[(tp + ranks - hop) % ranks, rows_of(c), 0, :] = zr[0, hop, c]
+            rollout[(tp + ranks - hop) % ranks, rows_of(c), 1, :] = zr[1, hop, c]
 
     def body(s, carry):
         @pl.when(s + AHEAD < chunks)
@@ -243,26 +234,35 @@
         def _():
             update(s - 1)
 
-        @pl.when(s >= 2)
+        @pl.when((s >= 2) & (s < chunks + 2))
         def _():
             spread(s - 2)
 
+        @pl.when(s >= 3)
+        def _():
+            merge(s - 3)
+
         return carry
 
-    lax.fori_loop(0, chunks + 2, body, 0)
+    lax.fori_loop(0, chunks + 3, body, 0)
 
     def drain(c, carry):
-        for copy in first_stage(c) + second_stage(c) + publish(c):
+        for copy in first_stage(c) + second_stage(c) + [publish(c, hop) for hop in range(1, ranks)]:
             copy.wait_send()
         for hop in range(ranks):
-            away, keep = forward(c, hop)
-            away.wait_send()
-            keep.wait()
-            arrived(c, hop).wait_recv()
+            forward(c, hop).wait_send()
         return carry
 
     lax.fori_loop(0, chunks, drain, 0)
-    wait(store_new(chunks - 2) + store_new(chunks - 1))
+
+
+def flush(*refs):
+    count = (len(refs) - 1) // 2
+    copies = [pltpu.make_async_copy(refs[i], refs[count + i], refs[-1].at[i]) for i in range(count)]
+    for copy in copies:
+        copy.start()
+    for copy in copies:
+        copy.wait()
 
 
 def shards(grad_parts, master, first_moment, second_moment, adam_step, rank_map):
@@ -278,12 +278,12 @@
     smem, anywhere = pl.BlockSpec(memory_space=pltpu.SMEM), pl.BlockSpec(memory_space=pl.ANY)
     vmem, dma = pltpu.VMEM, pltpu.SemaphoreType.DMA
     short, brain, single = jnp.int16, jnp.bfloat16, jnp.float32
-    *outs, both = pl.pallas_call(
+    held = [vmem(s.shape, s.dtype) for s in states] + [vmem((ranks, row_count, 2, width), brain)]
+    results = pl.pallas_call(
         functools.partial(kernel, ranks),
-        out_shape=[jax.ShapeDtypeStruct(s.shape, s.dtype) for s in states]
-        + [jax.ShapeDtypeStruct((2, ranks, row_count, width), brain)],
+        out_shape=held,
         in_specs=[smem, smem] + [anywhere] * 4,
-        out_specs=[anywhere] * 4,
+        out_specs=[pl.BlockSpec(memory_space=pltpu.VMEM)] * 4,
         scratch_shapes=[
             vmem((chunks, 2, ROWS, half), brain),
             vmem((chunks, 2, ROWS, half), brain),
@@ -295,12 +295,11 @@
             vmem((chunks, ROWS, half), short),
             vmem((chunks, 8, 128), single),
             vmem((chunks, 8, 128), single),
-            vmem((chunks, ranks, ROWS, width), brain),
-            vmem((ranks, chunks, ROWS, width), brain),
+            vmem((chunks, ranks - 1, ROWS, width), brain),
+            vmem((2, ranks, chunks, ROWS, width), brain),
             vmem((2, ROWS, columns), brain),
             vmem((2, ROWS, half), brain),
             vmem((2, ROWS, half), brain),
-            vmem((2, 3, ROWS, columns), single),
             vmem((2, 3, ROWS, columns), single),
             vmem((ranks, ROWS, width), brain),
             dma((chunks, 4)),
@@ -314,16 +313,22 @@
             dma((2,)),
             dma((2, 2)),
             dma((2, 3)),
-            dma((2, 3)),
-            dma((chunks, ranks)),
         ],
         compiler_params=pltpu.CompilerParams(
-            collective_id=0, has_side_effects=True, vmem_limit_bytes=48 * 1024 * 1024
+            collective_id=0, has_side_effects=True, vmem_limit_bytes=32 * 1024 * 1024
         ),
         name="exchange",
     )(order, scales, grad, *states)
-    rollout = jnp.transpose(both, (1, 2, 0, 3)).reshape(ranks, row_count, 2, 1, width)
-    return (*(o.reshape(master.shape) for o in outs), rollout)
+    *outs, rollout = pl.pallas_call(
+        flush,
+        out_shape=[jax.ShapeDtypeStruct(r.shape, r.dtype) for r in results],
+        in_specs=[anywhere] * 4,
+        out_specs=[anywhere] * 4,
+        scratch_shapes=[dma((4,))],
+        compiler_params=pltpu.CompilerParams(vmem_limit_bytes=1024 * 1024),
+        name="flush",
+    )(*results)
+    return (*(o.reshape(master.shape) for o in outs), rollout.reshape(ranks, row_count, 2, 1, width))
 
 
 def solution(mesh):

time: 178 us -> 157 us (0.88)
  local copies, waits for them, and re-layouts: 28.6 us -> 0.58 us
  Pallas kernels: 147 us -> 153 us
    unnamed x12 -> x0, local copies, waits for them, and re-layouts: 28.5 us -> none
    pallas_call x1 -> x2, Pallas kernels: 147 us -> 153 us  [the longest x1 143 us: shards(): pl.pallas_call(functools.partial(kernel, ranks), out_shape=held, in_specs...]
where the time goes in v1:
time: 157 us; the launch traced here: 156 us
  Pallas kernels  153 us (97%)
    pallas_call x1, Pallas kernels, shards(): pl.pallas_call(functools.partial(kernel, ranks), out_shape=held, in_specs...  143 us
    pallas_call x1, Pallas kernels, shards(): pl.pallas_call(flush, out_shape=[jax.ShapeDtypeStruct(r.shape, r.dtype) f...  9.92 us

profile of v1, /device:TPU:0, one launch (start us, length us, event | category | flops | bytes accessed | tf_op | source)
XLA Modules:
  0.0 156.4 jit_solution(6813002954220473152)
XLA Ops:
  1.4 0.6 pad_maximum_fusion.scales
  2.0 0.8 pad_add_fusion
  2.8 0.6 dynamic_slice.3.order
  3.4 143.0 %exchange.1 = (f32[256,7168]{1,0:T(8,128)S(1)}, f32[256,7168]{1,0:T(8,128)S(1)}, f32[256,7168]{1,0:T(8,128)S(1)}, bf16[4,256,2,1792]{3,2,1,0:T(2,128)(2,1)S(1)}) custom-call(s32[4]{0:T(128)} %dynamic_slice.3.order, f32[2]{0:T(128)} %pad_maximum_fusion.scales, bf16[4,256,7168]{2,1,0:T(8,128)(2,1)} %bitcast.10, f32[256,7168]{1,0:T(8,128)} %bitcast.11, ...), custom_call_target="tpu_custom_call" | custom-call | tf_op jit(solution)/shard_map/exchange/pallas_call | solution.py:282
  146.4 9.9 %flush.1 = (f32[256,7168]{1,0:T(8,128)}, f32[256,7168]{1,0:T(8,128)}, f32[256,7168]{1,0:T(8,128)}, bf16[4,256,2,1792]{3,2,1,0:T(2,128)(2,1)}) custom-call(f32[256,7168]{1,0:T(8,128)S(1)} %get-tuple-element.12.refs_0_, f32[256,7168]{1,0:T(8,128)S(1)} %get-tuple-element.13.refs_1_, f32[256,7168]{1,0:T(8,128)S(1)} %get-tuple-element.14.refs_2_, ...), custom_call_target="tpu_custom_call" | custom-call | tf_op jit(solution)/shard_map/flush/pallas_call | solution.py:322

commit v2 on v1

v2 whole, which is shorter than its diff:
```python
import functools
import math
import types
import jax
import jax.numpy as jnp
from jax import lax
from jax.experimental import pallas as pl
from jax.experimental.pallas import tpu as pltpu
from jax.sharding import PartitionSpec as P

beta_one = 0.9
beta_two = 0.95
rate_value = 0.001
decay_value = 0.01
eps_value = 1e-08

ROWS = 16
TAIL = 8
FAR, NEAR = 2, 1
UPDATE, SPREAD, MERGE = 1, 3, 4
STRIP = 256
TOP = 32767.0
TINY = 1e-30
MESH = pl.DeviceIdType.MESH


def corrections(adam_step):
    count = adam_step[0].astype(jnp.float32)
    return 1.0 - jnp.power(beta_one, count), 1.0 - jnp.power(beta_two, count)


def plain_shards(grad_parts, master, first_moment, second_moment, adam_step, rank_map):
    summed = lax.psum_scatter(grad_parts.astype(jnp.float32), "dp", scatter_dimension=2, tiled=True)
    summed = summed.reshape(master.shape)
    fix_one, fix_two = corrections(adam_step)
    new_first = beta_one * first_moment + (1.0 - beta_one) * summed
    new_second = beta_two * second_moment + (1.0 - beta_two) * summed * summed
    first_hat = new_first / fix_one
    second_hat = new_second / fix_two
    new_master = master - rate_value * (
        first_hat / (jnp.sqrt(second_hat) + eps_value) + decay_value * master
    )
    row_count = master.shape[1]
    ranks = lax.axis_size("tp")
    block_width = master.shape[2] // ranks
    piece = new_master.astype(jnp.bfloat16).reshape(1, row_count, 1, ranks, block_width)
    ordered = jnp.take(piece, rank_map, axis=3)
    placed = lax.all_to_all(ordered, "tp", split_axis=3, concat_axis=0, tiled=True)
    rollout = lax.all_gather(placed, "eng", axis=2, tiled=True)
    return (new_master, new_first, new_second, rollout)


def stacked(value, times, axis):
    return jnp.concatenate([value] * times, axis=axis) if times > 1 else value


def pack_sum(near, far, packed, scale):
    rows, tiles = packed.shape[0], packed.shape[1] // 128
    tops = [jnp.zeros((8, 128), jnp.float32) for _ in range(4)]
    for tile in range(tiles):
        columns = pl.ds(tile * 128, 128)
        size = jnp.abs(near[:, columns].astype(jnp.float32) + far[:, columns].astype(jnp.float32))
        for part in range(rows // 8):
            slot = (2 * tile + part) % 4
            tops[slot] = jnp.maximum(tops[slot], size[8 * part : 8 * part + 8])
    top = jnp.maximum(jnp.maximum(tops[0], tops[1]), jnp.maximum(tops[2], tops[3]))
    top = jnp.maximum(jnp.max(top, axis=0, keepdims=True), TINY)
    scale[...] = top * (1.0 / TOP)
    factor = jnp.broadcast_to(TOP / top, (rows, 128))
    for tile in range(tiles):
        columns = pl.ds(tile * 128, 128)
        value = near[:, columns].astype(jnp.float32) + far[:, columns].astype(jnp.float32)
        packed[:, columns] = jnp.round(value * factor).astype(jnp.int32).astype(jnp.int16)


def kernel(ranks, names, rank_map, adam_step, grad, master, first, second, *refs):
    new_master, new_first, new_second, rollout = refs[:4]
    body_refs, tail_refs = refs[4 : 4 + len(names)], refs[4 + len(names) :]
    columns = grad.shape[2]
    half = columns // 2
    width = columns // ranks
    me, tp, eng = (lax.axis_index(a) for a in ("dp", "tp", "eng"))
    at_x = me + 1 - 2 * (me % 2)
    at_y = (me + 2) % 4
    at_d = 3 - me
    barrier = pltpu.get_barrier_semaphore()
    for where in (
        [{"dp": at_x}, {"dp": at_y}, {"eng": 1 - eng}] + [{"tp": (tp + hop) % ranks} for hop in range(1, ranks)]
    ):
        pl.semaphore_signal(barrier, inc=1, device_id=where, device_id_type=MESH)
    left, right = pl.ds(0, half), pl.ds(half, half)
    states = (master, first, second)
    main = types.SimpleNamespace(**dict(zip(names, body_refs)), base=0, start=0)
    main.chunks, main.rows = main.rxa.shape[0], main.rxa.shape[2]
    tail = types.SimpleNamespace(**dict(zip(names, tail_refs)), base=main.chunks * main.rows, start=main.chunks)
    tail.chunks, tail.rows = tail.rxa.shape[0], tail.rxa.shape[2]
    def rows_of(g, c):
        return pl.ds(pl.multiple_of(g.base + c * g.rows, 8), g.rows)

    def remote(src, dst, send, recv, **where):
        return pltpu.make_async_remote_copy(
            src_ref=src, dst_ref=dst, send_sem=send, recv_sem=recv, device_id=where, device_id_type=MESH
        )

    def far_x(g, c):
        return remote(grad.at[at_d, rows_of(g, c), left], g.rxa.at[c, 1], g.p1_send.at[c, 0], g.p1_recv.at[c, 0], dp=at_x)

    def far_y(g, c):
        return remote(grad.at[at_d, rows_of(g, c), right], g.rxb.at[c, 1], g.p1_send.at[c, 1], g.p1_recv.at[c, 1], dp=at_y)

    def near_x(g, c):
        return remote(grad.at[at_x, rows_of(g, c), left], g.rxa.at[c, 0], g.p1_send.at[c, 2], g.p1_recv.at[c, 2], dp=at_x)

    def near_y(g, c):
        return remote(grad.at[at_y, rows_of(g, c), right], g.rxb.at[c, 0], g.p1_send.at[c, 3], g.p1_recv.at[c, 3], dp=at_y)

    def sum_y(g, c):
        return remote(g.txa.at[c], g.r2a.at[c], g.p2_send.at[c, 0], g.p2_recv.at[c, 0], dp=at_y)

    def unit_y(g, c):
        return remote(g.tsa.at[c], g.rsa.at[c], g.p2_send.at[c, 1], g.p2_recv.at[c, 1], dp=at_y)

    def sum_x(g, c):
        return remote(g.txb.at[c], g.r2b.at[c], g.p2_send.at[c, 2], g.p2_recv.at[c, 2], dp=at_x)

    def unit_x(g, c):
        return remote(g.tsb.at[c], g.rsb.at[c], g.p2_send.at[c, 3], g.p2_recv.at[c, 3], dp=at_x)

    def publish(g, c, hop):
        return remote(
            g.zs.at[c, hop - 1], g.zr.at[eng, hop, c], g.z_send.at[c, hop], g.z_recv.at[c, hop], tp=(tp + hop) % ranks
        )

    def forward(g, c, hop):
        block = g.zr.at[eng, hop, c]
        return remote(block, block, g.f_send.at[c, hop], g.f_recv.at[c, hop], eng=1 - eng)

    def arrival(g, c, hop):
        block = g.zr.at[1 - eng, hop, c]
        return remote(block, block, g.f_send.at[c, hop], g.f_recv.at[c, hop], eng=1 - eng)

    def load_own(g, c):
        return [pltpu.make_async_copy(grad.at[me, rows_of(g, c)], g.own.at[c % 2], g.own_sem.at[c % 2])]

    def load_side(g, c):
        rows = rows_of(g, c)
        return [
            pltpu.make_async_copy(grad.at[at_y, rows, left], g.side_a.at[c % 2], g.side_sem.at[c % 2, 0]),
            pltpu.make_async_copy(grad.at[at_x, rows, right], g.side_b.at[c % 2], g.side_sem.at[c % 2, 1]),
        ]

    def load_old(g, c):
        return [
            pltpu.make_async_copy(states[i].at[rows_of(g, c)], g.old.at[c % 2, i], g.old_sem.at[c % 2, i])
            for i in range(3)
        ]

    def start(copies):
        for copy in copies:
            copy.start()

    def wait(copies):
        for copy in copies:
            copy.wait()

    pl.semaphore_wait(barrier, 2 + ranks)
    for c in range(FAR):
        start([far_x(main, c), far_y(main, c)])
        if c < NEAR:
            start([near_x(main, c), near_y(main, c)])
    for c in range(2):
        start(load_side(main, c) + load_own(main, c) + load_old(main, c))
    for c in range(tail.chunks):
        start(load_side(tail, c) + load_own(tail, c) + load_old(tail, c))

    count = jnp.full((1, 128), adam_step[0], jnp.int32).astype(jnp.float32)
    scale_one = 1.0 / (1.0 - jnp.exp(count * math.log(beta_one)))
    scale_two = 1.0 / (1.0 - jnp.exp(count * math.log(beta_two)))

    def reduce_side(g, c):
        slot = c % 2
        wait(load_side(g, c))
        far_x(g, c).wait_recv()
        pack_sum(g.side_a.at[slot], g.rxa.at[c, 1], g.txa.at[c], g.tsa.at[c])
        start([sum_y(g, c), unit_y(g, c)])
        far_y(g, c).wait_recv()
        pack_sum(g.side_b.at[slot], g.rxb.at[c, 1], g.txb.at[c], g.tsb.at[c])
        start([sum_x(g, c), unit_x(g, c)])

        @pl.when(c + 2 < g.chunks)
        def _():
            start(load_side(g, c + 2))

    def update(g, c):
        slot, rows = c % 2, rows_of(g, c)
        wait(load_own(g, c) + load_old(g, c))
        for copy in (near_x, near_y, sum_y, unit_y, sum_x, unit_x):
            copy(g, c).wait_recv()

        def spread_out(value):
            return stacked(jnp.broadcast_to(value, (g.rows, 128)), STRIP // 128, 1)

        one, two = spread_out(scale_one), spread_out(scale_two)
        unit_a, unit_b = spread_out(g.rsa[c]), spread_out(g.rsb[c])
        for strip in range(columns // STRIP):
            at = pl.ds(strip * STRIP, STRIP)
            side = strip * STRIP // half
            inner = pl.ds(strip * STRIP - side * half, STRIP)
            got, sums, unit = ((g.rxa, g.r2a, unit_a), (g.rxb, g.r2b, unit_b))[side]
            summed = g.own[slot, :, at].astype(jnp.float32) + got[c, 0, :, inner].astype(jnp.float32)
            summed += sums[c, :, inner].astype(jnp.int32).astype(jnp.float32) * unit
            first_now = beta_one * g.old[slot, 1, :, at] + (1.0 - beta_one) * summed
            second_now = beta_two * g.old[slot, 2, :, at] + (1.0 - beta_two) * summed * summed
            was = g.old[slot, 0, :, at]
            step = (first_now * one) / (jnp.sqrt(second_now * two) + eps_value)
            now = was - rate_value * (step + decay_value * was)
            new_master[rows, at] = now
            new_first[rows, at] = first_now
            new_second[rows, at] = second_now
            block = strip * STRIP // width
            g.held[block, :, pl.ds(strip * STRIP - block * width, STRIP)] = now.astype(jnp.bfloat16)
        for hop in range(1, ranks):
            g.zs[c, hop - 1] = g.held[rank_map[(tp + hop) % ranks]]
            publish(g, c, hop).start()
        g.zr[eng, 0, c] = g.held[rank_map[tp]]
        forward(g, c, 0).start()

        @pl.when(c + 2 < g.chunks)
        def _():
            start(load_own(g, c + 2) + load_old(g, c + 2))

    def spread(g, c):
        for hop in range(1, ranks):
            publish(g, c, hop).wait_recv()
            forward(g, c, hop).start()

    def merge(g, c):
        for hop in range(ranks):
            arrival(g, c, hop).wait_recv()
            for part in range(2):
                rollout[(tp + ranks - hop) % ranks, rows_of(g, c), part, :] = g.zr[part, hop, c]

    def at_step(s, lag, act):
        for g in (main, tail):
            c = s - lag - g.start

            @pl.when((c >= 0) & (c < g.chunks))
            def _():
                act(g, c)

    def send_far(g, c):
        start([far_x(g, c), far_y(g, c)])

    def send_near(g, c):
        start([near_x(g, c), near_y(g, c)])

    def drain(g, c):
        for copy in (far_x, far_y, near_x, near_y, sum_y, unit_y, sum_x, unit_x):
            copy(g, c).wait_send()
        for hop in range(ranks):
            forward(g, c, hop).wait_send()
            if hop:
                publish(g, c, hop).wait_send()

    def body(s, carry):
        at_step(s, 0, reduce_side)
        at_step(s, -FAR, send_far)
        at_step(s, -NEAR, send_near)
        at_step(s, UPDATE, update)
        at_step(s, SPREAD, spread)
        at_step(s, MERGE, merge)
        at_step(s, MERGE + 1, drain)
        return carry

    lax.fori_loop(0, main.chunks + tail.chunks + MERGE + 1, body, 0)


def flush(*refs):
    count = (len(refs) - 1) // 2
    copies = [pltpu.make_async_copy(refs[i], refs[count + i], refs[-1].at[i]) for i in range(count)]
    for copy in copies:
        copy.start()
    for copy in copies:
        copy.wait()


def shards(grad_parts, master, first_moment, second_moment, adam_step, rank_map):
    replicas, ranks = lax.axis_size("dp"), lax.axis_size("tp")
    row_count, columns = master.shape[1], master.shape[2]
    half, width = columns // 2, columns // ranks
    grad = grad_parts.reshape(replicas, row_count, columns)
    states = [s.reshape(row_count, columns) for s in (master, first_moment, second_moment)]
    smem, anywhere = pl.BlockSpec(memory_space=pltpu.SMEM), pl.BlockSpec(memory_space=pl.ANY)
    vmem, dma = pltpu.VMEM, pltpu.SemaphoreType.DMA
    short, brain, single = jnp.int16, jnp.bfloat16, jnp.float32

    def scratch(chunks, rows):
        shapes = {name: vmem((chunks, 2, rows, half), brain) for name in ("rxa", "rxb")}
        shapes |= {name: vmem((chunks, rows, half), short) for name in ("txa", "txb", "r2a", "r2b")}
        shapes |= {name: vmem((chunks, 1, 128), single) for name in ("tsa", "tsb", "rsa", "rsb")}
        shapes["zs"] = vmem((chunks, ranks - 1, rows, width), brain)
        shapes["zr"] = vmem((2, ranks, chunks, rows, width), brain)
        shapes["own"] = vmem((2, rows, columns), brain)
        shapes |= {name: vmem((2, rows, half), brain) for name in ("side_a", "side_b")}
        shapes["old"] = vmem((2, 3, rows, columns), single)
        shapes["held"] = vmem((ranks, rows, width), brain)
        shapes |= {name: dma((chunks, 4)) for name in ("p1_send", "p1_recv", "p2_send", "p2_recv")}
        shapes |= {name: dma((chunks, ranks)) for name in ("z_send", "z_recv", "f_send", "f_recv")}
        shapes |= {"own_sem": dma((2,)), "side_sem": dma((2, 2)), "old_sem": dma((2, 3))}
        return shapes

    main = scratch(row_count // ROWS - 1, ROWS)
    tail = scratch(ROWS // TAIL, TAIL)
    results = pl.pallas_call(
        functools.partial(kernel, ranks, tuple(main)),
        out_shape=[vmem(s.shape, s.dtype) for s in states] + [vmem((ranks, row_count, 2, width), brain)],
        in_specs=[smem, smem] + [anywhere] * 4,
        out_specs=[pl.BlockSpec(memory_space=pltpu.VMEM)] * 4,
        scratch_shapes=[*main.values(), *tail.values()],
        compiler_params=pltpu.CompilerParams(
            collective_id=0, has_side_effects=True, vmem_limit_bytes=34 * 1024 * 1024
        ),
        name="exchange",
    )(rank_map, adam_step, grad, *states)
    *outs, rollout = pl.pallas_call(
        flush,
        out_shape=[jax.ShapeDtypeStruct(r.shape, r.dtype) for r in results],
        in_specs=[anywhere] * 4,
        out_specs=[anywhere] * 4,
        scratch_shapes=[dma((4,))],
        compiler_params=pltpu.CompilerParams(vmem_limit_bytes=1024 * 1024),
        name="flush",
    )(*results)
    return (*(o.reshape(master.shape) for o in outs), rollout.reshape(ranks, row_count, 2, 1, width))


def solution(mesh):
    sizes = dict(mesh.shape)

    def step(grad_parts, master, *rest):
        columns = master.shape[2] // sizes["eng"]
        width = columns // sizes["tp"]
        rows = master.shape[1] // sizes["dp"]
        fits = sizes["dp"] == 4 and sizes["eng"] == 2 and width % STRIP == 0 and (columns // 2) % STRIP == 0
        fits = fits and rows % ROWS == 0 and rows // ROWS > FAR + 1
        return jax.shard_map(
            shards if fits else plain_shards,
            mesh=mesh,
            in_specs=(
                P("dp", "tp", None, "eng"),
                P("tp", "dp", "eng"),
                P("tp", "dp", "eng"),
                P("tp", "dp", "eng"),
                P(),
                P(),
            ),
            out_specs=(
                P("tp", "dp", "eng"),
                P("tp", "dp", "eng"),
                P("tp", "dp", "eng"),
                P(None, "dp", None, "tp", None),
            ),
            check_vma=False,
        )(grad_parts, master, *rest)

    return step
```

time: 157 us -> 148 us (0.943)
  Pallas kernels: 153 us -> 147 us
    pallas_call x1, Pallas kernels: 143 us -> 137 us  [shards(): pl.pallas_call(functools.partial(kernel, ranks, tuple(main)), out_shape=[...]
where the time goes in v2:
time: 148 us
  Pallas kernels  147 us (99%)
    pallas_call x1, Pallas kernels, shards(): pl.pallas_call(functools.partial(kernel, ranks, tuple(main)), out_shape=[...  137 us
    pallas_call x1, Pallas kernels, shards(): pl.pallas_call(flush, out_shape=[jax.ShapeDtypeStruct(r.shape, r.dtype) f...  9.92 us

profile of v2, /device:TPU:0, one launch (start us, length us, event | category | flops | bytes accessed | tf_op | source)
XLA Modules:
  0.0 148.0 jit_solution(7778741133423630254)
XLA Ops:
  1.3 136.8 %exchange.1 = (f32[256,7168]{1,0:T(8,128)S(1)}, f32[256,7168]{1,0:T(8,128)S(1)}, f32[256,7168]{1,0:T(8,128)S(1)}, bf16[4,256,2,1792]{3,2,1,0:T(2,128)(2,1)S(1)}) custom-call(s32[4]{0:T(128)} %rank_map.1, s32[1]{0:T(128)S(6)} %copy.11.adam_step, bf16[4,256,7168]{2,1,0:T(8,128)(2,1)} %bitcast.10, f32[256,7168]{1,0:T(8,128)} %bitcast.11, f32[256,7168]{1,0:T(8,128)} %bitcast.12, ...), custom_call_target="tpu_custom_call" | custom-call | tf_op jit(solution)/shard_map/exchange/pallas_call | solution.py:314
  138.1 9.9 %flush.1 = (f32[256,7168]{1,0:T(8,128)}, f32[256,7168]{1,0:T(8,128)}, f32[256,7168]{1,0:T(8,128)}, bf16[4,256,2,1792]{3,2,1,0:T(2,128)(2,1)}) custom-call(f32[256,7168]{1,0:T(8,128)S(1)} %get-tuple-element.12.refs_0_, f32[256,7168]{1,0:T(8,128)S(1)} %get-tuple-element.13.refs_1_, f32[256,7168]{1,0:T(8,128)S(1)} %get-tuple-element.14.refs_2_, ...), custom_call_target="tpu_custom_call" | custom-call | tf_op jit(solution)/shard_map/flush/pallas_call | solution.py:325

commit v3 on v2

--- a/solution.py
+++ b/solution.py
@@ -103,41 +103,38 @@
         )
 
     def far_x(g, c):
-        return remote(grad.at[at_d, rows_of(g, c), left], g.rxa.at[c, 1], g.p1_send.at[c, 0], g.p1_recv.at[c, 0], dp=at_x)
+        return remote(grad.at[at_d, rows_of(g, c), left], g.rxa.at[c, 1], g.sent.at[0], g.far_sem.at[c], dp=at_x)
 
     def far_y(g, c):
-        return remote(grad.at[at_d, rows_of(g, c), right], g.rxb.at[c, 1], g.p1_send.at[c, 1], g.p1_recv.at[c, 1], dp=at_y)
+        return remote(grad.at[at_d, rows_of(g, c), right], g.rxb.at[c, 1], g.sent.at[1], g.far_sem.at[c], dp=at_y)
 
     def near_x(g, c):
-        return remote(grad.at[at_x, rows_of(g, c), left], g.rxa.at[c, 0], g.p1_send.at[c, 2], g.p1_recv.at[c, 2], dp=at_x)
+        return remote(grad.at[at_x, rows_of(g, c), left], g.rxa.at[c, 0], g.sent.at[0], g.mid_sem.at[c], dp=at_x)
 
     def near_y(g, c):
-        return remote(grad.at[at_y, rows_of(g, c), right], g.rxb.at[c, 0], g.p1_send.at[c, 3], g.p1_recv.at[c, 3], dp=at_y)
+        return remote(grad.at[at_y, rows_of(g, c), right], g.rxb.at[c, 0], g.sent.at[1], g.mid_sem.at[c], dp=at_y)
 
     def sum_y(g, c):
-        return remote(g.txa.at[c], g.r2a.at[c], g.p2_send.at[c, 0], g.p2_recv.at[c, 0], dp=at_y)
+        return remote(g.txa.at[c], g.r2a.at[c], g.sent.at[2], g.mid_sem.at[c], dp=at_y)
+
+    def sum_x(g, c):
+        return remote(g.txb.at[c], g.r2b.at[c], g.sent.at[2], g.mid_sem.at[c], dp=at_x)
 
     def unit_y(g, c):
-        return remote(g.tsa.at[c], g.rsa.at[c], g.p2_send.at[c, 1], g.p2_recv.at[c, 1], dp=at_y)
-
-    def sum_x(g, c):
-        return remote(g.txb.at[c], g.r2b.at[c], g.p2_send.at[c, 2], g.p2_recv.at[c, 2], dp=at_x)
+        return remote(g.ts.at[c, 0], g.rs.at[c, 0], g.sent.at[3], g.unit_sem.at[c], dp=at_y)
 
     def unit_x(g, c):
-        return remote(g.tsb.at[c], g.rsb.at[c], g.p2_send.at[c, 3], g.p2_recv.at[c, 3], dp=at_x)
+        return remote(g.ts.at[c, 1], g.rs.at[c, 1], g.sent.at[3], g.unit_sem.at[c], dp=at_x)
 
     def publish(g, c, hop):
-        return remote(
-            g.zs.at[c, hop - 1], g.zr.at[eng, hop, c], g.z_send.at[c, hop], g.z_recv.at[c, hop], tp=(tp + hop) % ranks
-        )
+        return remote(g.zs.at[c, hop - 1], g.zr.at[eng, hop, c], g.sent.at[4], g.z_sem.at[c], tp=(tp + hop) % ranks)
 
     def forward(g, c, hop):
         block = g.zr.at[eng, hop, c]
-        return remote(block, block, g.f_send.at[c, hop], g.f_recv.at[c, hop], eng=1 - eng)
-
-    def arrival(g, c, hop):
-        block = g.zr.at[1 - eng, hop, c]
-        return remote(block, block, g.f_send.at[c, hop], g.f_recv.at[c, hop], eng=1 - eng)
+        return remote(block, block, g.sent.at[5], g.f_sem.at[c], eng=1 - eng)
+
+    def wait_bytes(like, sem):
+        pltpu.make_async_copy(like, like, sem).wait()
 
     def load_own(g, c):
         return [pltpu.make_async_copy(grad.at[me, rows_of(g, c)], g.own.at[c % 2], g.own_sem.at[c % 2])]
@@ -180,11 +177,10 @@
     def reduce_side(g, c):
         slot = c % 2
         wait(load_side(g, c))
-        far_x(g, c).wait_recv()
-        pack_sum(g.side_a.at[slot], g.rxa.at[c, 1], g.txa.at[c], g.tsa.at[c])
+        wait_bytes(g.rxa.at[c], g.far_sem.at[c])
+        pack_sum(g.side_a.at[slot], g.rxa.at[c, 1], g.txa.at[c], g.ts.at[c, 0])
         start([sum_y(g, c), unit_y(g, c)])
-        far_y(g, c).wait_recv()
-        pack_sum(g.side_b.at[slot], g.rxb.at[c, 1], g.txb.at[c], g.tsb.at[c])
+        pack_sum(g.side_b.at[slot], g.rxb.at[c, 1], g.txb.at[c], g.ts.at[c, 1])
         start([sum_x(g, c), unit_x(g, c)])
 
         @pl.when(c + 2 < g.chunks)
@@ -194,14 +190,14 @@
     def update(g, c):
         slot, rows = c % 2, rows_of(g, c)
         wait(load_own(g, c) + load_old(g, c))
-        for copy in (near_x, near_y, sum_y, unit_y, sum_x, unit_x):
-            copy(g, c).wait_recv()
+        wait_bytes(g.own, g.mid_sem.at[c])
+        wait_bytes(g.rs.at[c], g.unit_sem.at[c])
 
         def spread_out(value):
             return stacked(jnp.broadcast_to(value, (g.rows, 128)), STRIP // 128, 1)
 
         one, two = spread_out(scale_one), spread_out(scale_two)
-        unit_a, unit_b = spread_out(g.rsa[c]), spread_out(g.rsb[c])
+        unit_a, unit_b = spread_out(g.rs[c, 0]), spread_out(g.rs[c, 1])
         for strip in range(columns // STRIP):
             at = pl.ds(strip * STRIP, STRIP)
             side = strip * STRIP // half
@@ -230,13 +226,13 @@
             start(load_own(g, c + 2) + load_old(g, c + 2))
 
     def spread(g, c):
+        wait_bytes(g.zs.at[c], g.z_sem.at[c])
         for hop in range(1, ranks):
-            publish(g, c, hop).wait_recv()
             forward(g, c, hop).start()
 
     def merge(g, c):
+        wait_bytes(g.zr.at[1 - eng, :, c], g.f_sem.at[c])
         for hop in range(ranks):
-            arrival(g, c, hop).wait_recv()
             for part in range(2):
                 rollout[(tp + ranks - hop) % ranks, rows_of(g, c), part, :] = g.zr[part, hop, c]
 
@@ -253,14 +249,6 @@
 
     def send_near(g, c):
         start([near_x(g, c), near_y(g, c)])
-
-    def drain(g, c):
-        for copy in (far_x, far_y, near_x, near_y, sum_y, unit_y, sum_x, unit_x):
-            copy(g, c).wait_send()
-        for hop in range(ranks):
-            forward(g, c, hop).wait_send()
-            if hop:
-                publish(g, c, hop).wait_send()
 
     def body(s, carry):
         at_step(s, 0, reduce_side)
@@ -269,10 +257,12 @@
         at_step(s, UPDATE, update)
         at_step(s, SPREAD, spread)
         at_step(s, MERGE, merge)
-        at_step(s, MERGE + 1, drain)
         return carry
 
-    lax.fori_loop(0, main.chunks + tail.chunks + MERGE + 1, body, 0)
+    lax.fori_loop(0, main.chunks + tail.chunks + MERGE, body, 0)
+    for g in (main, tail):
+        for i, like in enumerate((g.rxa, g.rxb, g.rxa, g.ts, g.zs, g.zr.at[eng])):
+            wait_bytes(like, g.sent.at[i])
 
 
 def flush(*refs):
@@ -297,15 +287,15 @@
     def scratch(chunks, rows):
         shapes = {name: vmem((chunks, 2, rows, half), brain) for name in ("rxa", "rxb")}
         shapes |= {name: vmem((chunks, rows, half), short) for name in ("txa", "txb", "r2a", "r2b")}
-        shapes |= {name: vmem((chunks, 1, 128), single) for name in ("tsa", "tsb", "rsa", "rsb")}
+        shapes |= {name: vmem((chunks, 2, 1, 128), single) for name in ("ts", "rs")}
         shapes["zs"] = vmem((chunks, ranks - 1, rows, width), brain)
         shapes["zr"] = vmem((2, ranks, chunks, rows, width), brain)
         shapes["own"] = vmem((2, rows, columns), brain)
         shapes |= {name: vmem((2, rows, half), brain) for name in ("side_a", "side_b")}
         shapes["old"] = vmem((2, 3, rows, columns), single)
         shapes["held"] = vmem((ranks, rows, width), brain)
-        shapes |= {name: dma((chunks, 4)) for name in ("p1_send", "p1_recv", "p2_send", "p2_recv")}
-        shapes |= {name: dma((chunks, ranks)) for name in ("z_send", "z_recv", "f_send", "f_recv")}
+        shapes |= {name: dma((chunks,)) for name in ("far_sem", "mid_sem", "unit_sem", "z_sem", "f_sem")}
+        shapes["sent"] = dma((6,))
         shapes |= {"own_sem": dma((2,)), "side_sem": dma((2, 2)), "old_sem": dma((2, 3))}
         return shapes
 

time: 148 us -> 144 us (0.973)
  Pallas kernels: 147 us -> 143 us
    pallas_call x1, Pallas kernels: 137 us -> 133 us  [shards(): pl.pallas_call(functools.partial(kernel, ranks, tuple(main)), out_shape=[...]
where the time goes in v3:
time: 144 us
  Pallas kernels  143 us (99%)
    pallas_call x1, Pallas kernels, shards(): pl.pallas_call(functools.partial(kernel, ranks, tuple(main)), out_shape=[...  133 us
    pallas_call x1, Pallas kernels, shards(): pl.pallas_call(flush, out_shape=[jax.ShapeDtypeStruct(r.shape, r.dtype) f...  9.92 us

profile of v3, /device:TPU:0, one launch (start us, length us, event | category | flops | bytes accessed | tf_op | source)
XLA Modules:
  0.0 144.0 jit_solution(11348355943956552969)
XLA Ops:
  1.3 132.8 %exchange.1 = (f32[256,7168]{1,0:T(8,128)S(1)}, f32[256,7168]{1,0:T(8,128)S(1)}, f32[256,7168]{1,0:T(8,128)S(1)}, bf16[4,256,2,1792]{3,2,1,0:T(2,128)(2,1)S(1)}) custom-call(s32[4]{0:T(128)} %rank_map.1, s32[1]{0:T(128)S(6)} %copy.11.adam_step, bf16[4,256,7168]{2,1,0:T(8,128)(2,1)} %bitcast.10, f32[256,7168]{1,0:T(8,128)} %bitcast.11, f32[256,7168]{1,0:T(8,128)} %bitcast.12, ...), custom_call_target="tpu_custom_call" | custom-call | tf_op jit(solution)/shard_map/exchange/pallas_call | solution.py:304
  134.1 9.9 %flush.1 = (f32[256,7168]{1,0:T(8,128)}, f32[256,7168]{1,0:T(8,128)}, f32[256,7168]{1,0:T(8,128)}, bf16[4,256,2,1792]{3,2,1,0:T(2,128)(2,1)}) custom-call(f32[256,7168]{1,0:T(8,128)S(1)} %get-tuple-element.12.refs_0_, f32[256,7168]{1,0:T(8,128)S(1)} %get-tuple-element.13.refs_1_, f32[256,7168]{1,0:T(8,128)S(1)} %get-tuple-element.14.refs_2_, ...), custom_call_target="tpu_custom_call" | custom-call | tf_op jit(solution)/shard_map/flush/pallas_call | solution.py:315

commit v4 on v3

--- a/solution.py
+++ b/solution.py
@@ -17,6 +17,7 @@
 ROWS = 16
 TAIL = 8
 FAR, NEAR = 2, 1
+RING = 8
 UPDATE, SPREAD, MERGE = 1, 3, 4
 STRIP = 256
 TOP = 32767.0
@@ -73,9 +74,9 @@
         packed[:, columns] = jnp.round(value * factor).astype(jnp.int32).astype(jnp.int16)
 
 
-def kernel(ranks, names, rank_map, adam_step, grad, master, first, second, *refs):
-    new_master, new_first, new_second, rollout = refs[:4]
-    body_refs, tail_refs = refs[4 : 4 + len(names)], refs[4 + len(names) :]
+def kernel(ranks, names, rank_map_in, adam_step_in, grad, master, first, second, *refs):
+    new_master, new_first, new_second, rollout, rank_map, adam_step, small_sem = refs[:7]
+    body_refs, tail_refs = refs[7 : 7 + len(names)], refs[7 + len(names) :]
     columns = grad.shape[2]
     half = columns // 2
     width = columns // ranks
@@ -103,62 +104,56 @@
         )
 
     def far_x(g, c):
-        return remote(grad.at[at_d, rows_of(g, c), left], g.rxa.at[c, 1], g.sent.at[0], g.far_sem.at[c], dp=at_x)
+        return remote(grad.at[at_d, rows_of(g, c), left], g.rxa.at[c, 1], g.sent.at[0], g.far_sem.at[c % RING], dp=at_x)
 
     def far_y(g, c):
-        return remote(grad.at[at_d, rows_of(g, c), right], g.rxb.at[c, 1], g.sent.at[1], g.far_sem.at[c], dp=at_y)
+        return remote(grad.at[at_d, rows_of(g, c), right], g.rxb.at[c, 1], g.sent.at[1], g.far_sem.at[c % RING], dp=at_y)
 
     def near_x(g, c):
-        return remote(grad.at[at_x, rows_of(g, c), left], g.rxa.at[c, 0], g.sent.at[0], g.mid_sem.at[c], dp=at_x)
+        return remote(grad.at[at_x, rows_of(g, c), left], g.rxa.at[c, 0], g.sent.at[0], g.mid_sem.at[c % RING], dp=at_x)
 
     def near_y(g, c):
-        return remote(grad.at[at_y, rows_of(g, c), right], g.rxb.at[c, 0], g.sent.at[1], g.mid_sem.at[c], dp=at_y)
+        return remote(grad.at[at_y, rows_of(g, c), right], g.rxb.at[c, 0], g.sent.at[1], g.mid_sem.at[c % RING], dp=at_y)
 
     def sum_y(g, c):
-        return remote(g.txa.at[c], g.r2a.at[c], g.sent.at[2], g.mid_sem.at[c], dp=at_y)
+        return remote(g.txa.at[c], g.r2a.at[c], g.sent.at[2], g.mid_sem.at[c % RING], dp=at_y)
 
     def sum_x(g, c):
-        return remote(g.txb.at[c], g.r2b.at[c], g.sent.at[2], g.mid_sem.at[c], dp=at_x)
+        return remote(g.txb.at[c], g.r2b.at[c], g.sent.at[2], g.mid_sem.at[c % RING], dp=at_x)
 
     def unit_y(g, c):
-        return remote(g.ts.at[c, 0], g.rs.at[c, 0], g.sent.at[3], g.unit_sem.at[c], dp=at_y)
+        return remote(g.ts.at[c, 0], g.rs.at[c, 0], g.sent.at[3], g.unit_sem.at[c % RING], dp=at_y)
 
     def unit_x(g, c):
-        return remote(g.ts.at[c, 1], g.rs.at[c, 1], g.sent.at[3], g.unit_sem.at[c], dp=at_x)
+        return remote(g.ts.at[c, 1], g.rs.at[c, 1], g.sent.at[3], g.unit_sem.at[c % RING], dp=at_x)
 
     def publish(g, c, hop):
-        return remote(g.zs.at[c, hop - 1], g.zr.at[eng, hop, c], g.sent.at[4], g.z_sem.at[c], tp=(tp + hop) % ranks)
+        return remote(g.zs.at[c, hop - 1], g.zr.at[eng, hop, c], g.sent.at[4], g.z_sem.at[c % RING], tp=(tp + hop) % ranks)
 
     def forward(g, c, hop):
         block = g.zr.at[eng, hop, c]
-        return remote(block, block, g.sent.at[5], g.f_sem.at[c], eng=1 - eng)
+        return remote(block, block, g.sent.at[5], g.f_sem.at[c % RING], eng=1 - eng)
 
     def wait_bytes(like, sem):
         pltpu.make_async_copy(like, like, sem).wait()
 
+    def load_side(g, c):
+        rows, sem = rows_of(g, c), g.load_sem.at[0, c % 2]
+        return [
+            pltpu.make_async_copy(grad.at[at_y, rows, left], g.side.at[c % 2, 0], sem),
+            pltpu.make_async_copy(grad.at[at_x, rows, right], g.side.at[c % 2, 1], sem),
+        ]
+
     def load_own(g, c):
-        return [pltpu.make_async_copy(grad.at[me, rows_of(g, c)], g.own.at[c % 2], g.own_sem.at[c % 2])]
-
-    def load_side(g, c):
-        rows = rows_of(g, c)
-        return [
-            pltpu.make_async_copy(grad.at[at_y, rows, left], g.side_a.at[c % 2], g.side_sem.at[c % 2, 0]),
-            pltpu.make_async_copy(grad.at[at_x, rows, right], g.side_b.at[c % 2], g.side_sem.at[c % 2, 1]),
-        ]
+        return [pltpu.make_async_copy(grad.at[me, rows_of(g, c)], g.own.at[c % 2], g.load_sem.at[1, c % 2])]
 
     def load_old(g, c):
-        return [
-            pltpu.make_async_copy(states[i].at[rows_of(g, c)], g.old.at[c % 2, i], g.old_sem.at[c % 2, i])
-            for i in range(3)
-        ]
+        sem = g.load_sem.at[2, c % 2]
+        return [pltpu.make_async_copy(states[i].at[rows_of(g, c)], g.old.at[c % 2, i], sem) for i in range(3)]
 
     def start(copies):
         for copy in copies:
             copy.start()
-
-    def wait(copies):
-        for copy in copies:
-            copy.wait()
 
     pl.semaphore_wait(barrier, 2 + ranks)
     for c in range(FAR):
@@ -170,17 +165,24 @@
     for c in range(tail.chunks):
         start(load_side(tail, c) + load_own(tail, c) + load_old(tail, c))
 
+    small = [
+        pltpu.make_async_copy(rank_map_in, rank_map, small_sem.at[0]),
+        pltpu.make_async_copy(adam_step_in, adam_step, small_sem.at[1]),
+    ]
+    start(small)
+    for copy in small:
+        copy.wait()
     count = jnp.full((1, 128), adam_step[0], jnp.int32).astype(jnp.float32)
     scale_one = 1.0 / (1.0 - jnp.exp(count * math.log(beta_one)))
     scale_two = 1.0 / (1.0 - jnp.exp(count * math.log(beta_two)))
 
     def reduce_side(g, c):
         slot = c % 2
-        wait(load_side(g, c))
-        wait_bytes(g.rxa.at[c], g.far_sem.at[c])
-        pack_sum(g.side_a.at[slot], g.rxa.at[c, 1], g.txa.at[c], g.ts.at[c, 0])
+        wait_bytes(g.side.at[slot], g.load_sem.at[0, slot])
+        wait_bytes(g.rxa.at[c], g.far_sem.at[c % RING])
+        pack_sum(g.side.at[slot, 0], g.rxa.at[c, 1], g.txa.at[c], g.ts.at[c, 0])
         start([sum_y(g, c), unit_y(g, c)])
-        pack_sum(g.side_b.at[slot], g.rxb.at[c, 1], g.txb.at[c], g.ts.at[c, 1])
+        pack_sum(g.side.at[slot, 1], g.rxb.at[c, 1], g.txb.at[c], g.ts.at[c, 1])
         start([sum_x(g, c), unit_x(g, c)])
 
         @pl.when(c + 2 < g.chunks)
@@ -189,9 +191,10 @@
 
     def update(g, c):
         slot, rows = c % 2, rows_of(g, c)
-        wait(load_own(g, c) + load_old(g, c))
-        wait_bytes(g.own, g.mid_sem.at[c])
-        wait_bytes(g.rs.at[c], g.unit_sem.at[c])
+        wait_bytes(g.own.at[slot], g.load_sem.at[1, slot])
+        wait_bytes(g.old.at[slot], g.load_sem.at[2, slot])
+        wait_bytes(g.own, g.mid_sem.at[c % RING])
+        wait_bytes(g.rs.at[c], g.unit_sem.at[c % RING])
 
         def spread_out(value):
             return stacked(jnp.broadcast_to(value, (g.rows, 128)), STRIP // 128, 1)
@@ -226,12 +229,12 @@
             start(load_own(g, c + 2) + load_old(g, c + 2))
 
     def spread(g, c):
-        wait_bytes(g.zs.at[c], g.z_sem.at[c])
+        wait_bytes(g.zs.at[c], g.z_sem.at[c % RING])
         for hop in range(1, ranks):
             forward(g, c, hop).start()
 
     def merge(g, c):
-        wait_bytes(g.zr.at[1 - eng, :, c], g.f_sem.at[c])
+        wait_bytes(g.zr.at[1 - eng, :, c], g.f_sem.at[c % RING])
         for hop in range(ranks):
             for part in range(2):
                 rollout[(tp + ranks - hop) % ranks, rows_of(g, c), part, :] = g.zr[part, hop, c]
@@ -280,7 +283,7 @@
     half, width = columns // 2, columns // ranks
     grad = grad_parts.reshape(replicas, row_count, columns)
     states = [s.reshape(row_count, columns) for s in (master, first_moment, second_moment)]
-    smem, anywhere = pl.BlockSpec(memory_space=pltpu.SMEM), pl.BlockSpec(memory_space=pl.ANY)
+    anywhere = pl.BlockSpec(memory_space=pl.ANY)
     vmem, dma = pltpu.VMEM, pltpu.SemaphoreType.DMA
     short, brain, single = jnp.int16, jnp.bfloat16, jnp.float32
 
@@ -291,12 +294,12 @@
         shapes["zs"] = vmem((chunks, ranks - 1, rows, width), brain)
         shapes["zr"] = vmem((2, ranks, chunks, rows, width), brain)
         shapes["own"] = vmem((2, rows, columns), brain)
-        shapes |= {name: vmem((2, rows, half), brain) for name in ("side_a", "side_b")}
+        shapes["side"] = vmem((2, 2, rows, half), brain)
         shapes["old"] = vmem((2, 3, rows, columns), single)
         shapes["held"] = vmem((ranks, rows, width), brain)
-        shapes |= {name: dma((chunks,)) for name in ("far_sem", "mid_sem", "unit_sem", "z_sem", "f_sem")}
+        shapes |= {name: dma((min(chunks, RING),)) for name in ("far_sem", "mid_sem", "unit_sem", "z_sem", "f_sem")}
         shapes["sent"] = dma((6,))
-        shapes |= {"own_sem": dma((2,)), "side_sem": dma((2, 2)), "old_sem": dma((2, 3))}
+        shapes["load_sem"] = dma((3, 2))
         return shapes
 
     main = scratch(row_count // ROWS - 1, ROWS)
@@ -304,9 +307,15 @@
     results = pl.pallas_call(
         functools.partial(kernel, ranks, tuple(main)),
         out_shape=[vmem(s.shape, s.dtype) for s in states] + [vmem((ranks, row_count, 2, width), brain)],
-        in_specs=[smem, smem] + [anywhere] * 4,
+        in_specs=[anywhere] * 6,
         out_specs=[pl.BlockSpec(memory_space=pltpu.VMEM)] * 4,
-        scratch_shapes=[*main.values(), *tail.values()],
+        scratch_shapes=[
+            pltpu.SMEM(rank_map.shape, rank_map.dtype),
+            pltpu.SMEM(adam_step.shape, adam_step.dtype),
+            dma((2,)),
+            *main.values(),
+            *tail.values(),
+        ],
         compiler_params=pltpu.CompilerParams(
             collective_id=0, has_side_effects=True, vmem_limit_bytes=34 * 1024 * 1024
         ),

time: 144 us -> 143 us (level)
  no operation moved by 1% of the time
where the time goes in v4:
time: 143 us
  Pallas kernels  142 us (99%)
    pallas_call x1, Pallas kernels, shards(): pl.pallas_call(functools.partial(kernel, ranks, tuple(main)), out_shape=[...  132 us
    pallas_call x1, Pallas kernels, shards(): pl.pallas_call(flush, out_shape=[jax.ShapeDtypeStruct(r.shape, r.dtype) f...  9.92 us

profile of v4, /device:TPU:0, one launch (start us, length us, event | category | flops | bytes accessed | tf_op | source)
XLA Modules:
  0.0 143.0 jit_solution(1107379297944879753)
XLA Ops:
  1.3 131.8 %exchange.1 = (f32[256,7168]{1,0:T(8,128)S(1)}, f32[256,7168]{1,0:T(8,128)S(1)}, f32[256,7168]{1,0:T(8,128)S(1)}, bf16[4,256,2,1792]{3,2,1,0:T(2,128)(2,1)S(1)}) custom-call(s32[4]{0:T(128)} %rank_map_in.1, s32[1]{0:T(128)S(6)} %copy.11.adam_step_in, bf16[4,256,7168]{2,1,0:T(8,128)(2,1)} %bitcast.10, f32[256,7168]{1,0:T(8,128)} %bitcast.11, ...), custom_call_target="tpu_custom_call" | custom-call | tf_op jit(solution)/shard_map/exchange/pallas_call | solution.py:307
  133.0 9.9 %flush.1 = (f32[256,7168]{1,0:T(8,128)}, f32[256,7168]{1,0:T(8,128)}, f32[256,7168]{1,0:T(8,128)}, bf16[4,256,2,1792]{3,2,1,0:T(2,128)(2,1)}) custom-call(f32[256,7168]{1,0:T(8,128)S(1)} %get-tuple-element.12.refs_0_, f32[256,7168]{1,0:T(8,128)S(1)} %get-tuple-element.13.refs_1_, f32[256,7168]{1,0:T(8,128)S(1)} %get-tuple-element.14.refs_2_, ...), custom_call_target="tpu_custom_call" | custom-call | tf_op jit(solution)/shard_map/flush/pallas_call | solution.py:324

commit v5 on v4

--- a/solution.py
+++ b/solution.py
@@ -18,7 +18,7 @@
 TAIL = 8
 FAR, NEAR = 2, 1
 RING = 8
-UPDATE, SPREAD, MERGE = 1, 3, 4
+UPDATE, SPREAD, MERGE = 1, 4, 5
 STRIP = 256
 TOP = 32767.0
 TINY = 1e-30
@@ -104,35 +104,35 @@
         )
 
     def far_x(g, c):
-        return remote(grad.at[at_d, rows_of(g, c), left], g.rxa.at[c, 1], g.sent.at[0], g.far_sem.at[c % RING], dp=at_x)
+        return remote(grad.at[at_d, rows_of(g, c), left], g.rxa.at[c, 1], g.sent.at[0], main.far_sem.at[(g.start + c) % RING], dp=at_x)
 
     def far_y(g, c):
-        return remote(grad.at[at_d, rows_of(g, c), right], g.rxb.at[c, 1], g.sent.at[1], g.far_sem.at[c % RING], dp=at_y)
+        return remote(grad.at[at_d, rows_of(g, c), right], g.rxb.at[c, 1], g.sent.at[1], main.far_sem.at[(g.start + c) % RING], dp=at_y)
 
     def near_x(g, c):
-        return remote(grad.at[at_x, rows_of(g, c), left], g.rxa.at[c, 0], g.sent.at[0], g.mid_sem.at[c % RING], dp=at_x)
+        return remote(grad.at[at_x, rows_of(g, c), left], g.rxa.at[c, 0], g.sent.at[0], main.mid_sem.at[(g.start + c) % RING], dp=at_x)
 
     def near_y(g, c):
-        return remote(grad.at[at_y, rows_of(g, c), right], g.rxb.at[c, 0], g.sent.at[1], g.mid_sem.at[c % RING], dp=at_y)
+        return remote(grad.at[at_y, rows_of(g, c), right], g.rxb.at[c, 0], g.sent.at[1], main.mid_sem.at[(g.start + c) % RING], dp=at_y)
 
     def sum_y(g, c):
-        return remote(g.txa.at[c], g.r2a.at[c], g.sent.at[2], g.mid_sem.at[c % RING], dp=at_y)
+        return remote(g.txa.at[c], g.r2a.at[c], g.sent.at[2], main.mid_sem.at[(g.start + c) % RING], dp=at_y)
 
     def sum_x(g, c):
-        return remote(g.txb.at[c], g.r2b.at[c], g.sent.at[2], g.mid_sem.at[c % RING], dp=at_x)
+        return remote(g.txb.at[c], g.r2b.at[c], g.sent.at[2], main.mid_sem.at[(g.start + c) % RING], dp=at_x)
 
     def unit_y(g, c):
-        return remote(g.ts.at[c, 0], g.rs.at[c, 0], g.sent.at[3], g.unit_sem.at[c % RING], dp=at_y)
+        return remote(g.ts.at[c, 0], g.rs.at[c, 0], g.sent.at[3], main.unit_sem.at[(g.start + c) % RING], dp=at_y)
 
     def unit_x(g, c):
-        return remote(g.ts.at[c, 1], g.rs.at[c, 1], g.sent.at[3], g.unit_sem.at[c % RING], dp=at_x)
+        return remote(g.ts.at[c, 1], g.rs.at[c, 1], g.sent.at[3], main.unit_sem.at[(g.start + c) % RING], dp=at_x)
 
     def publish(g, c, hop):
-        return remote(g.zs.at[c, hop - 1], g.zr.at[eng, hop, c], g.sent.at[4], g.z_sem.at[c % RING], tp=(tp + hop) % ranks)
+        return remote(g.zs.at[c, hop - 1], g.zr.at[eng, hop, c], g.sent.at[4], main.z_sem.at[(g.start + c) % RING], tp=(tp + hop) % ranks)
 
     def forward(g, c, hop):
         block = g.zr.at[eng, hop, c]
-        return remote(block, block, g.sent.at[5], g.f_sem.at[c % RING], eng=1 - eng)
+        return remote(block, block, g.sent.at[5], main.f_sem.at[(g.start + c) % RING], eng=1 - eng)
 
     def wait_bytes(like, sem):
         pltpu.make_async_copy(like, like, sem).wait()
@@ -162,7 +162,7 @@
             start([near_x(main, c), near_y(main, c)])
     for c in range(2):
         start(load_side(main, c) + load_own(main, c) + load_old(main, c))
-    for c in range(tail.chunks):
+    for c in range(2):
         start(load_side(tail, c) + load_own(tail, c) + load_old(tail, c))
 
     small = [
@@ -179,7 +179,7 @@
     def reduce_side(g, c):
         slot = c % 2
         wait_bytes(g.side.at[slot], g.load_sem.at[0, slot])
-        wait_bytes(g.rxa.at[c], g.far_sem.at[c % RING])
+        wait_bytes(g.rxa.at[c], main.far_sem.at[(g.start + c) % RING])
         pack_sum(g.side.at[slot, 0], g.rxa.at[c, 1], g.txa.at[c], g.ts.at[c, 0])
         start([sum_y(g, c), unit_y(g, c)])
         pack_sum(g.side.at[slot, 1], g.rxb.at[c, 1], g.txb.at[c], g.ts.at[c, 1])
@@ -193,8 +193,8 @@
         slot, rows = c % 2, rows_of(g, c)
         wait_bytes(g.own.at[slot], g.load_sem.at[1, slot])
         wait_bytes(g.old.at[slot], g.load_sem.at[2, slot])
-        wait_bytes(g.own, g.mid_sem.at[c % RING])
-        wait_bytes(g.rs.at[c], g.unit_sem.at[c % RING])
+        wait_bytes(g.own, main.mid_sem.at[(g.start + c) % RING])
+        wait_bytes(g.rs.at[c], main.unit_sem.at[(g.start + c) % RING])
 
         def spread_out(value):
             return stacked(jnp.broadcast_to(value, (g.rows, 128)), STRIP // 128, 1)
@@ -229,12 +229,12 @@
             start(load_own(g, c + 2) + load_old(g, c + 2))
 
     def spread(g, c):
-        wait_bytes(g.zs.at[c], g.z_sem.at[c % RING])
+        wait_bytes(g.zs.at[c], main.z_sem.at[(g.start + c) % RING])
         for hop in range(1, ranks):
             forward(g, c, hop).start()
 
     def merge(g, c):
-        wait_bytes(g.zr.at[1 - eng, :, c], g.f_sem.at[c % RING])
+        wait_bytes(g.zr.at[1 - eng, :, c], main.f_sem.at[(g.start + c) % RING])
         for hop in range(ranks):
             for part in range(2):
                 rollout[(tp + ranks - hop) % ranks, rows_of(g, c), part, :] = g.zr[part, hop, c]
@@ -302,8 +302,9 @@
         shapes["load_sem"] = dma((3, 2))
         return shapes
 
-    main = scratch(row_count // ROWS - 1, ROWS)
-    tail = scratch(ROWS // TAIL, TAIL)
+    main = scratch(row_count // ROWS - 2, ROWS)
+    tail = scratch(2 * ROWS // TAIL, TAIL)
+    tail |= {name: dma((1,)) for name in ("far_sem", "mid_sem", "unit_sem", "z_sem", "f_sem")}
     results = pl.pallas_call(
         functools.partial(kernel, ranks, tuple(main)),
         out_shape=[vmem(s.shape, s.dtype) for s in states] + [vmem((ranks, row_count, 2, width), brain)],
@@ -341,7 +342,7 @@
         width = columns // sizes["tp"]
         rows = master.shape[1] // sizes["dp"]
         fits = sizes["dp"] == 4 and sizes["eng"] == 2 and width % STRIP == 0 and (columns // 2) % STRIP == 0
-        fits = fits and rows % ROWS == 0 and rows // ROWS > FAR + 1
+        fits = fits and rows % ROWS == 0 and rows // ROWS > FAR + 2
         return jax.shard_map(
             shards if fits else plain_shards,
             mesh=mesh,

time: 143 us -> 142 us (level)
  no operation moved by 1% of the time
where the time goes in v5:
time: 142 us
  Pallas kernels  141 us (99%)
    pallas_call x1, Pallas kernels, shards(): pl.pallas_call(functools.partial(kernel, ranks, tuple(main)), out_shape=[...  131 us
    pallas_call x1, Pallas kernels, shards(): pl.pallas_call(flush, out_shape=[jax.ShapeDtypeStruct(r.shape, r.dtype) f...  9.92 us

profile of v5, /device:TPU:0, one launch (start us, length us, event | category | flops | bytes accessed | tf_op | source)
XLA Modules:
  0.0 142.3 jit_solution(4265253618178506104)
XLA Ops:
  1.3 131.1 %exchange.1 = (f32[256,7168]{1,0:T(8,128)S(1)}, f32[256,7168]{1,0:T(8,128)S(1)}, f32[256,7168]{1,0:T(8,128)S(1)}, bf16[4,256,2,1792]{3,2,1,0:T(2,128)(2,1)S(1)}) custom-call(s32[4]{0:T(128)} %rank_map_in.1, s32[1]{0:T(128)S(6)} %copy.11.adam_step_in, bf16[4,256,7168]{2,1,0:T(8,128)(2,1)} %bitcast.10, f32[256,7168]{1,0:T(8,128)} %bitcast.11, ...), custom_call_target="tpu_custom_call" | custom-call | tf_op jit(solution)/shard_map/exchange/pallas_call | solution.py:308
  132.3 9.9 %flush.1 = (f32[256,7168]{1,0:T(8,128)}, f32[256,7168]{1,0:T(8,128)}, f32[256,7168]{1,0:T(8,128)}, bf16[4,256,2,1792]{3,2,1,0:T(2,128)(2,1)}) custom-call(f32[256,7168]{1,0:T(8,128)S(1)} %get-tuple-element.12.refs_0_, f32[256,7168]{1,0:T(8,128)S(1)} %get-tuple-element.13.refs_1_, f32[256,7168]{1,0:T(8,128)S(1)} %get-tuple-element.14.refs_2_, ...), custom_call_target="tpu_custom_call" | custom-call | tf_op jit(solution)/shard_map/flush/pallas_call | solution.py:325
